TPU v7x, 32 devices: a whole 2x2x4 slice. The times are simulated.
32 devices in a mesh: outer: 2 (over core), dp: 4 (over z), tensor: 4 (over y, x).
Axes of the slice: x: 2, y: 2, z: 4, core: 2. Of those that a mesh axis runs over, the one named last changes fastest.
Arguments:
- attn: bfloat16 [2048, 8192], P(('outer', 'dp'), 'tensor'), may hold values from -6 to 6
- out_weight: bfloat16 [8192, 8192], P(None, 'tensor'), may hold values from -0.0625 to 0.0625
- resid: bfloat16 [2048, 8192], P(('outer', 'dp'), 'tensor'), may hold values from -8 to 8
- norm_gain: bfloat16 [8192], P('tensor'), may hold values from 0.5 to 1.5
- head: bfloat16 [8192], P('tensor'), may hold values from -1 to 1
- lengths: int32 [32], P(('outer', 'dp')), may hold values from 1 to 64
- pairs: int32 [32, 2], P(('outer', 'dp')), may hold values from 0 to 3, as said below
- pair_valid: int32 [32], P(('outer', 'dp')), may hold values from 0 to 1, as said below
- loss_scale: float32 [1], replicated, may hold values from 1024 to 8192
Outputs:
- loss: float32 [1], replicated
- grad_out_proj: float32 [8192, 8192], P(('outer', 'dp'), 'tensor')
- grad_gain: float32 [8192], P('tensor')
- grad_head: float32 [8192], P('tensor')
Inputs may be any that keep to these rules, and one draw needn't show every extreme that they name: `pairs`: in each pair the two numbers differ; the first pair of each replica is valid. `pair_valid`: the first of each replica's 4 entries is 1.
All inputs are finite; a program needn't handle non-finite values.
Results may differ from a plain program's by a relative error of at most 0.003.
Values may be sent and summed in bfloat16 or wider, within the bound.
A program may use at most 128 MiB of HBM per device.

v0:
```python
import jax
import jax.numpy as jnp
from jax import lax
from jax.sharding import PartitionSpec as P


def shards(attn, out_weight, resid, norm_gain, head, lengths, pairs, pair_valid, loss_scale):
    f32 = jnp.float32
    tok_dev = attn.shape[0]
    feats = resid.shape[1]
    tensor = lax.axis_size("tensor")
    width = feats * tensor
    seqs_dev = lengths.shape[0]
    seq_len = tok_dev // seqs_dev
    valid = pair_valid.astype(f32)
    count = lax.psum(jnp.sum(valid), ("outer", "dp"))
    part = lax.dot_general(out_weight, attn, (((1,), (1,)), ((), ())), preferred_element_type=f32)
    part = part.astype(jnp.bfloat16).reshape(tensor, feats, tok_dev)
    part = lax.all_to_all(part, "tensor", split_axis=0, concat_axis=0, tiled=True)
    z = resid.astype(f32).T + jnp.sum(part.astype(f32), axis=0)
    gain = norm_gain.astype(f32)[:, None]
    headv = head.astype(f32)[:, None]
    both = headv * gain
    sums = lax.psum(jnp.stack([jnp.sum(z * z, axis=0), jnp.sum(z * both, axis=0)]), "tensor")
    inv = 1.0 / jnp.sqrt(sums[0] / width + 1e-05)
    score = sums[1] * inv
    position = jnp.arange(tok_dev)
    seq_of = position // seq_len
    within = position % seq_len
    member = (within[:, None] < lengths[None, :]) & (
        seq_of[:, None] == jnp.arange(seqs_dev)[None, :]
    )
    pooling = member.astype(f32) / lengths.astype(f32)[None, :]
    reward = jnp.sum(pooling * score[:, None], axis=0)
    choose = jnp.arange(seqs_dev)[None, :]
    select = (pairs[:, 0:1] == choose).astype(f32) - (pairs[:, 1:2] == choose).astype(f32)
    margin = jnp.sum(select * reward[None, :], axis=1)
    loss_part = jnp.sum(valid * jax.nn.softplus(-margin))
    dmargin = -loss_scale[0] * valid * jax.nn.sigmoid(-margin) / count
    dreward = jnp.sum(dmargin[:, None] * select, axis=0)
    dscore = jnp.sum(pooling * dreward[None, :], axis=1)
    weight = inv * dscore
    dproj = weight[None, :] * both - z * (inv**3 * dscore * sums[1] / width)[None, :]
    dproj = dproj.astype(jnp.bfloat16)
    zsum = jnp.sum(z * weight[None, :], axis=1)
    gathered = lax.all_gather(dproj, "tensor", axis=0, tiled=True)
    exchanged = lax.all_to_all(gathered, ("outer", "dp"), split_axis=0, concat_axis=1, tiled=True)
    grad_out_proj = jnp.dot(
        exchanged,
        lax.all_gather(attn, ("outer", "dp"), axis=0, tiled=True),
        preferred_element_type=f32,
    )
    zsum, loss_sum = lax.psum((zsum, loss_part), ("outer", "dp"))
    loss = (loss_sum / count).reshape(1)
    return (loss, grad_out_proj, zsum * headv[:, 0], zsum * gain[:, 0])


def solution(mesh):
    return jax.shard_map(
        shards,
        mesh=mesh,
        in_specs=(
            P(("outer", "dp"), "tensor"),
            P(None, "tensor"),
            P(("outer", "dp"), "tensor"),
            P("tensor"),
            P("tensor"),
            P(("outer", "dp")),
            P(("outer", "dp"), None),
            P(("outer", "dp")),
            P(),
        ),
        out_specs=(P(), P(("outer", "dp"), "tensor"), P("tensor"), P("tensor")),
        check_vma=False,
    )
```

profile of v0, /device:TPU:0, one launch (start us, length us, event | category | flops | bytes accessed | tf_op | source)
XLA Modules:
  0.0 368.8 jit_solution(16129040595212171715)
XLA Ops:
  7.2 16.7 %convolution_convert_fusion = bf16[8192,256]{1,0:T(8,128)(2,1)} fusion(bf16[8192,2048]{1,0:T(8,128)(2,1)} %param.10, bf16[256,2048]{1,0:T(8,128)(2,1)} %param.9), kind=kOutput, calls=%fused_computation | convolution fusion | flops 8592031744 | bytes 38797312 | tf_op jit(solution)/shard_map/dot_general | solution.py:17
  23.9 0.0 copy-start
  23.9 0.0 copy-start.3
  23.9 0.0 copy-start.5
  23.9 0.0 copy-start.1
  23.9 0.0 copy-start.2
  23.9 5.3 %all-to-all-start = ((bf16[4,2048,256]{2,1,0:T(8,128)(2,1)}), bf16[4,2048,256]{2,1,0:T(8,128)(2,1)}, u32[]{:S(2)}, u32[]{:S(2)}) async-start(bf16[4,2048,256]{2,1,0:T(8,128)(2,1)} %bitcast.31), calls=%async_computation | async-start | bytes 8388608 | tf_op jit(solution)/shard_map/all_to_all | solution.py:19
  29.3 0.0 all-gather.3.cloned.1.call-start
  29.3 0.0 copy-done
  29.3 0.5 copy.15
  29.8 0.0 copy-done.3
  30.5 0.0 copy-done.5
  30.5 0.0 copy-done.1
  30.5 0.0 copy-done.2
  30.6 0.0 copy-start.4
  30.6 47.4 %all-to-all-done = bf16[4,2048,256]{2,1,0:T(8,128)(2,1)} async-done(((bf16[4,2048,256]{2,1,0:T(8,128)(2,1)}), bf16[4,2048,256]{2,1,0:T(8,128)(2,1)}, u32[]{:S(2)}, u32[]{:S(2)}) %all-to-all-start) | async-done | bytes 4194336 | tf_op jit(solution)/shard_map/all_to_all | solution.py:19
  77.9 3.0 convert_reduce_fusion
  80.9 0.5 multiply_reduce_fusion.2
  81.4 8.9 %psum.28 = f32[2,256]{1,0:T(2,128)S(1)} all-reduce(f32[2,256]{1,0:T(2,128)S(1)} %pad_maximum_fusion), channel_id=1, replica_groups=mesh['outer'=2,'dp'=4,'tensor'=4] {'tensor'}, use_global_device_ids=true, to_apply=%region_3.0 | all-reduce | flops 512 | bytes 4096 | tf_op jit(solution)/shard_map/psum | solution.py:24
  90.3 0.2 multiply_reduce_fusion.4
  90.5 0.2 multiply_reduce_fusion.6
  90.7 0.0 copy-done.4
  90.7 0.6 convert_reduce_fusion.1
  91.3 16.2 %psum.30 = f32[]{:T(128)} all-reduce(f32[]{:T(128)} %get-tuple-element.6), channel_id=1, replica_groups=mesh['outer'=2,'dp'=4,'tensor'=4] {'outer','dp'}, use_global_device_ids=true, to_apply=%region_9.10 | all-reduce | flops 1 | bytes 8 | tf_op jit(solution)/shard_map/psum | solution.py:16
  107.5 0.7 fusion.9
  108.2 0.1 multiply_reduce_fusion.5
  108.3 0.1 multiply_reduce_fusion.3
  108.4 1.5 subtract_convert_fusion
  109.9 0.0 all-gather.3.cloned.1.call-update
  109.9 0.0 all-gather.5.cloned.1.call-start
  110.0 0.7 all-gather.5.cloned.1.call-update
  110.7 50.8 %all-gather.3.cloned.1.call-done = bf16[8192,256]{1,0:T(8,128)(2,1)} async-done(((bf16[2048,256]{1,0:T(8,128)(2,1)}), bf16[8192,256]{1,0:T(8,128)(2,1)}) %all-gather.3.cloned.1.call-update) | async-done | bytes 4194320 | tf_op jit(solution)/shard_map/all_gather | solution.py:46
  161.5 4.6 %all-to-all-start.1 = ((bf16[8,1024,256]{2,1,0:T(8,128)(2,1)}), bf16[8,1024,256]{2,1,0:T(8,128)(2,1)}, u32[]{:S(2)}, u32[]{:S(2)}) async-start(bf16[8,1024,256]{2,1,0:T(8,128)(2,1)} %bitcast.30), calls=%async_computation.1 | async-start | bytes 8388608 | tf_op jit(solution)/shard_map/all_to_all | solution.py:47
  166.1 171.7 %all-reduce = (f32[]{:T(128)}, f32[2048]{0:T(1024)S(1)}) all-reduce(f32[]{:T(128)} %get-tuple-element.7, f32[2048]{0:T(1024)S(1)} %get-tuple-element.11), channel_id=1, replica_groups=mesh['outer'=2,'dp'=4,'tensor'=4] {'outer','dp'}, use_global_device_ids=true, to_apply=%region_7.8 | all-reduce | flops 2049 | bytes 16392 | tf_op jit(solution)/shard_map/psum | solution.py:53
  339.1 0.6 convert_multiply_fusion
  339.7 0.0 all-to-all-done.1
  339.7 6.5 %copy.16 = bf16[1024,8,256]{0,2,1:T(8,128)(2,1)} copy(bf16[1024,8,256]{2,0,1:T(8,128)(2,1)} %bitcast.13) | data formatting | bytes 8388608 | tf_op jit(solution)/shard_map/all_to_all | solution.py:47
  346.2 0.0 all-gather.5.cloned.1.call-done
  346.2 14.6 %fusion.11 = f32[1024,2048]{1,0:T(8,128)} fusion(bf16[1024,2048]{0,1:T(8,128)(2,1)} %bitcast.32, bf16[2048,2048]{1,0:T(8,128)(2,1)} %all-gather.5.cloned.1.call-done), kind=kOutput, calls=%fused_computation.44 | convolution fusion | flops 8589934592 | bytes 20971520 | tf_op jit(solution)/shard_map/dot_general | solution.py:48
  (7 shorter events, 0.1 us)
Async XLA Ops:
  23.9 5.4 %copy-start = (bf16[256,2048]{1,0:T(8,128)(2,1)S(1)}, bf16[256,2048]{1,0:T(8,128)(2,1)}, u32[]{:S(2)}) copy-start(bf16[256,2048]{1,0:T(8,128)(2,1)} %param.11) | copy-start | bytes 3145732
  23.9 5.9 %copy-start.3 = (s32[4]{0:T(128)S(1)}, s32[4]{0:T(128)}, u32[]{:S(2)}) copy-start(s32[4]{0:T(128)} %param.14) | copy-start | bytes 52
  23.9 6.6 %copy-start.5 = (s32[4,2]{0,1:T(2,128)S(1)}, s32[4,2]{0,1:T(2,128)}, u32[]{:S(2)}) copy-start(s32[4,2]{0,1:T(2,128)} %param.15) | copy-start | bytes 100
  23.9 6.6 %copy-start.1 = (bf16[2048]{0:T(1024)(128)(2,1)S(1)}, bf16[2048]{0:T(1024)(128)(2,1)}, u32[]{:S(2)}) copy-start(bf16[2048]{0:T(1024)(128)(2,1)} %param.12) | copy-start | bytes 12292
  23.9 6.6 %copy-start.2 = (bf16[2048]{0:T(1024)(128)(2,1)S(1)}, bf16[2048]{0:T(1024)(128)(2,1)}, u32[]{:S(2)}) copy-start(bf16[2048]{0:T(1024)(128)(2,1)} %param.13) | copy-start | bytes 12292
  23.9 54.0 %all-to-all-start = ((bf16[4,2048,256]{2,1,0:T(8,128)(2,1)}), bf16[4,2048,256]{2,1,0:T(8,128)(2,1)}, u32[]{:S(2)}, u32[]{:S(2)}) async-start(bf16[4,2048,256]{2,1,0:T(8,128)(2,1)} %bitcast.31), calls=%async_computation | async-start | bytes 8388608 | tf_op jit(solution)/shard_map/all_to_all | solution.py:19
  29.3 132.2 %all-gather.3.cloned.1.call-start = ((), (), s32[]{:S(2)}) async-start(), calls=%async_computation.2 | async-start | bytes 5242880 | tf_op jit(solution)/shard_map/all_gather | solution.py:46
  30.6 60.2 %copy-start.4 = (s32[4]{0:T(128)S(1)}, s32[4]{0:T(128)}, u32[]{:S(2)}) copy-start(s32[4]{0:T(128)} %param.16) | copy-start | bytes 52
  109.9 236.3 %all-gather.5.cloned.1.call-start = ((), (), s32[]{:S(2)}) async-start(), calls=%async_computation.3 | async-start | bytes 9437184 | tf_op jit(solution)/shard_map/all_gather | solution.py:50
  161.5 178.2 %all-to-all-start.1 = ((bf16[8,1024,256]{2,1,0:T(8,128)(2,1)}), bf16[8,1024,256]{2,1,0:T(8,128)(2,1)}, u32[]{:S(2)}, u32[]{:S(2)}) async-start(bf16[8,1024,256]{2,1,0:T(8,128)(2,1)} %bitcast.30), calls=%async_computation.1 | async-start | bytes 8388608 | tf_op jit(solution)/shard_map/all_to_all | solution.py:47
Sparse Core Ops, SparseCore 0:
  110.0 51.4 all-gather.2
  163.1 160.7 all-gather.4
where the time goes:
time: 369 us
  blocking collectives  197 us (53%)
  waiting for transfers between devices  98.9 us (27%)
  matrix products  31.4 us (9%)
  between operations  17.3 us (5%)
  starting transfers between devices  9.99 us (3%)
  other arithmetic  7.44 us (2%)
  local copies, waits for them, and re-layouts  7.01 us (2%)
    psum x1, blocking collectives, shards(): zsum, loss_sum = lax.psum((zsum, loss_part), ('outer', 'dp'))  172 us
    all_gather x1, waiting for transfers between devices, shards(): gathered = lax.all_gather(dproj, 'tensor', axis=0, tiled=True)  50.8 us
    all_to_all x1, waiting for transfers between devices, shards(): lax.all_to_all(part, 'tensor', split_axis=0, concat_axis=0, tiled=True)  47.4 us
    dot_general x1, matrix products, shards(): lax.dot_general(out_weight, attn, (((1,), (1,)), ((), ())), preferred_ele...  16.7 us
    psum x1, blocking collectives, shards(): count = lax.psum(jnp.sum(valid), ('outer', 'dp'))  16.2 us
    dot_general x1, matrix products, shards(): jnp.dot(exchanged, lax.all_gather(attn, ('outer', 'dp'), axis=0, tiled=Tr...  14.6 us
    psum x1, blocking collectives, shards(): lax.psum(jnp.stack([jnp.sum(z * z, axis=0), jnp.sum(z * both, axis=0)]),...  8.91 us
  transfers between devices with their start and end apart: 4, of which 2 were waited for; matrix products, arithmetic and copies ran while one was open for 2% of the time, Pallas kernels for 0%

commit v1 on v0

--- a/solution.py
+++ b/solution.py
@@ -2,6 +2,16 @@
 import jax.numpy as jnp
 from jax import lax
 from jax.sharding import PartitionSpec as P
+from jax.lax import axis_index, axis_size, ppermute
+
+
+def group_follow(block_in, out_dim):
+    block_in = jnp.moveaxis(block_in, 0, out_dim)
+    b_now = block_in.shape
+    w1 = block_in.reshape(
+        *b_now[:out_dim], b_now[out_dim] * b_now[out_dim + 1], *b_now[out_dim + 2 :]
+    )
+    return w1
 
 
 def shards(attn, out_weight, resid, norm_gain, head, lengths, pairs, pair_valid, loss_scale):
@@ -43,7 +53,23 @@
     dproj = weight[None, :] * both - z * (inv**3 * dscore * sums[1] / width)[None, :]
     dproj = dproj.astype(jnp.bfloat16)
     zsum = jnp.sum(z * weight[None, :], axis=1)
-    gathered = lax.all_gather(dproj, "tensor", axis=0, tiled=True)
+    n_slots = axis_size("tensor")
+    gallery = tuple(((dev, (dev + 1) % n_slots) for dev in range(n_slots)))
+    column = tuple(((jj, m) for m, jj in gallery))
+    y_new, g_now = ([], [])
+    for hop_no in range(n_slots - 1):
+        if hop_no % 2 == 0:
+            mid_arr = ppermute(y_new[-1] if y_new else dproj, axis_name="tensor", perm=gallery)
+            y_new.append(mid_arr)
+        else:
+            h_now = ppermute(g_now[-1] if g_now else dproj, axis_name="tensor", perm=column)
+            g_now.append(h_now)
+    long_array = jnp.stack([*y_new[::-1], dproj, *g_now])
+    u_next = axis_index("tensor")
+    moved = len(y_new)
+    back = u_next - moved
+    long_array = long_array[(jnp.arange(n_slots) - back) % n_slots]
+    gathered = group_follow(long_array, 0)
     exchanged = lax.all_to_all(gathered, ("outer", "dp"), split_axis=0, concat_axis=1, tiled=True)
     grad_out_proj = jnp.dot(
         exchanged,

time: 369 us -> 335 us (0.908)
  blocking collectives: 197 us -> 134 us
  waiting for transfers between devices: 98.9 us -> 116 us
  local copies, waits for them, and re-layouts: 7.01 us -> 12 us
    ppermute x0 -> x3, waiting for transfers between devices: none -> 68.9 us  [the longest x2 46.6 us: shards(): ppermute(y_new[-1] if y_new else dproj, axis_name='tensor', perm=gallery)]
    psum x1, blocking collectives: 172 us -> 104 us  [shards(): zsum, loss_sum = lax.psum((zsum, loss_part), ('outer', 'dp'))]
    all_gather x1 -> x0, waiting for transfers between devices: 50.8 us -> none  [shards(): gathered = lax.all_gather(dproj, 'tensor', axis=0, tiled=True)]
    gather x0 -> x1, local copies, waits for them, and re-layouts: none -> 4.96 us  [shards(): long_array = long_array[(jnp.arange(n_slots) - back) % n_slots]]
    psum x1, blocking collectives: 16.2 us -> 20.6 us  [shards(): count = lax.psum(jnp.sum(valid), ('outer', 'dp'))]
  transfers between devices with their start and end apart: 4 -> 6, of which waited for: 2 -> 4; matrix products, arithmetic and copies ran while one was open for 2% -> 7% of each run, Pallas kernels for 0% -> 0%
where the time goes in v1:
time: 335 us; the launch traced here: 334 us
  blocking collectives  134 us (40%)
  waiting for transfers between devices  116 us (35%)
  matrix products  31.4 us (9%)
  between operations  17.3 us (5%)
  starting transfers between devices  12.9 us (4%)
  local copies, waits for them, and re-layouts  12 us (4%)
  other arithmetic  10.8 us (3%)
    psum x1, blocking collectives, shards(): zsum, loss_sum = lax.psum((zsum, loss_part), ('outer', 'dp'))  104 us
    ppermute x2, waiting for transfers between devices, shards(): ppermute(y_new[-1] if y_new else dproj, axis_name='tensor', perm=gallery)  46.6 us
    all_to_all x1, waiting for transfers between devices, shards(): lax.all_to_all(part, 'tensor', split_axis=0, concat_axis=0, tiled=True)  46.6 us
    ppermute x1, waiting for transfers between devices, shards(): ppermute(g_now[-1] if g_now else dproj, axis_name='tensor', perm=column)  22.4 us
    psum x1, blocking collectives, shards(): count = lax.psum(jnp.sum(valid), ('outer', 'dp'))  20.6 us
    dot_general x1, matrix products, shards(): lax.dot_general(out_weight, attn, (((1,), (1,)), ((), ())), preferred_ele...  16.7 us
    dot_general x1, matrix products, shards(): jnp.dot(exchanged, lax.all_gather(attn, ('outer', 'dp'), axis=0, tiled=Tr...  14.6 us
    psum x1, blocking collectives, shards(): lax.psum(jnp.stack([jnp.sum(z * z, axis=0), jnp.sum(z * both, axis=0)]),...  8.97 us
  transfers between devices with their start and end apart: 6, of which 4 were waited for; matrix products, arithmetic and copies ran while one was open for 7% of the time, Pallas kernels for 0%

profile of v1, /device:TPU:0, one launch (start us, length us, event | category | flops | bytes accessed | tf_op | source)
XLA Modules:
  0.0 334.3 jit_solution(6699907102236108869)
XLA Ops:
  7.2 16.7 %convolution_convert_fusion = bf16[8192,256]{1,0:T(8,128)(2,1)} fusion(bf16[8192,2048]{1,0:T(8,128)(2,1)} %param.10, bf16[256,2048]{1,0:T(8,128)(2,1)} %param.9), kind=kOutput, calls=%fused_computation.1 | convolution fusion | flops 8592031744 | bytes 38797312 | tf_op jit(solution)/shard_map/dot_general | solution.py:27
  23.9 0.0 copy-start
  23.9 0.0 copy-start.3
  23.9 0.0 copy-start.5
  23.9 0.0 copy-start.1
  23.9 0.0 copy-start.2
  23.9 5.3 %all-to-all-start = ((bf16[4,2048,256]{2,1,0:T(8,128)(2,1)}), bf16[4,2048,256]{2,1,0:T(8,128)(2,1)}, u32[]{:S(2)}, u32[]{:S(2)}) async-start(bf16[4,2048,256]{2,1,0:T(8,128)(2,1)} %bitcast.37), calls=%async_computation | async-start | bytes 8388608 | tf_op jit(solution)/shard_map/all_to_all | solution.py:29
  29.3 0.0 all-gather.2.cloned.1.call-start
  29.3 0.7 all-gather.2.cloned.1.call-update
  30.0 0.0 copy-done
  30.0 0.5 copy.16
  30.6 0.0 copy-done.3
  31.2 0.0 copy-done.5
  31.3 0.0 copy-done.1
  31.3 0.0 copy-done.2
  31.3 0.0 copy-start.4
  31.3 46.6 %all-to-all-done = bf16[4,2048,256]{2,1,0:T(8,128)(2,1)} async-done(((bf16[4,2048,256]{2,1,0:T(8,128)(2,1)}), bf16[4,2048,256]{2,1,0:T(8,128)(2,1)}, u32[]{:S(2)}, u32[]{:S(2)}) %all-to-all-start) | async-done | bytes 4194336 | tf_op jit(solution)/shard_map/all_to_all | solution.py:29
  77.9 3.0 convert_reduce_fusion
  80.9 0.4 multiply_reduce_fusion.2
  81.3 9.0 %psum.28 = f32[2,256]{1,0:T(2,128)S(1)} all-reduce(f32[2,256]{1,0:T(2,128)S(1)} %pad_maximum_fusion.1), channel_id=1, replica_groups=mesh['outer'=2,'dp'=4,'tensor'=4] {'tensor'}, use_global_device_ids=true, to_apply=%region_3.0 | all-reduce | flops 512 | bytes 4096 | tf_op jit(solution)/shard_map/psum | solution.py:34
  90.3 0.2 multiply_reduce_fusion.4
  90.5 0.2 multiply_reduce_fusion.6
  90.7 0.0 copy-done.4
  90.7 0.6 convert_reduce_fusion.1
  91.3 20.6 %psum.30 = f32[]{:T(128)} all-reduce(f32[]{:T(128)} %get-tuple-element.6), channel_id=1, replica_groups=mesh['outer'=2,'dp'=4,'tensor'=4] {'outer','dp'}, use_global_device_ids=true, to_apply=%region_9.10 | all-reduce | flops 1 | bytes 8 | tf_op jit(solution)/shard_map/psum | solution.py:26
  111.9 0.7 fusion.11
  112.5 0.1 multiply_reduce_fusion.5
  112.6 0.1 multiply_reduce_fusion.3
  112.7 1.5 subtract_convert_fusion
  114.3 0.0 collective-permute-start
  114.3 2.9 collective-permute-start.2
  117.2 24.0 %collective-permute-done = bf16[2048,256]{1,0:T(8,128)(2,1)S(1)} collective-permute-done((bf16[2048,256]{1,0:T(8,128)(2,1)}, bf16[2048,256]{1,0:T(8,128)(2,1)S(1)}, u32[]{:S(2)}, u32[]{:S(2)}) %collective-permute-start) | collective-permute-done | bytes 1048608 | tf_op jit(solution)/shard_map/ppermute | solution.py:62
  141.2 0.0 collective-permute-start.1
  141.3 22.4 %collective-permute-done.2 = bf16[2048,256]{1,0:T(8,128)(2,1)S(1)} collective-permute-done((bf16[2048,256]{1,0:T(8,128)(2,1)}, bf16[2048,256]{1,0:T(8,128)(2,1)S(1)}, u32[]{:S(2)}, u32[]{:S(2)}) %collective-permute-start.2) | collective-permute-done | bytes 1048608 | tf_op jit(solution)/shard_map/ppermute | solution.py:65
  163.6 22.6 %collective-permute-done.1 = bf16[2048,256]{1,0:T(8,128)(2,1)S(1)} collective-permute-done((bf16[2048,256]{1,0:T(8,128)(2,1)S(1)}, bf16[2048,256]{1,0:T(8,128)(2,1)S(1)}, u32[]{:S(2)}, u32[]{:S(2)}) %collective-permute-start.1) | collective-permute-done | bytes 1048608 | tf_op jit(solution)/shard_map/ppermute | solution.py:62
  186.2 3.3 pad_maximum_fusion
  189.5 5.0 %gather_fusion = bf16[4,2048,256]{2,1,0:T(8,128)(2,1)} fusion(bf16[4,2048,256]{2,1,0:T(8,128)(2,1)} %pad_maximum_fusion, s32[1024]{0:T(1024)S(1)} %pad_clamp_fusion), kind=kCustom, calls=%fused_computation | custom fusion | bytes 8388624 | tf_op jit(solution)/shard_map/gather | solution.py:71
  194.5 4.6 %all-to-all-start.1 = ((bf16[8,1024,256]{2,1,0:T(8,128)(2,1)}), bf16[8,1024,256]{2,1,0:T(8,128)(2,1)}, u32[]{:S(2)}, u32[]{:S(2)}) async-start(bf16[8,1024,256]{2,1,0:T(8,128)(2,1)} %bitcast.36), calls=%async_computation.1 | async-start | bytes 8388608 | tf_op jit(solution)/shard_map/all_to_all | solution.py:73
  199.1 104.2 %all-reduce = (f32[]{:T(128)}, f32[2048]{0:T(1024)S(1)}) all-reduce(f32[]{:T(128)} %get-tuple-element.7, f32[2048]{0:T(1024)S(1)} %get-tuple-element.11), channel_id=1, replica_groups=mesh['outer'=2,'dp'=4,'tensor'=4] {'outer','dp'}, use_global_device_ids=true, to_apply=%region_7.8 | all-reduce | flops 2049 | bytes 16392 | tf_op jit(solution)/shard_map/psum | solution.py:79
  304.6 0.6 convert_multiply_fusion
  305.2 0.0 all-to-all-done.1
  305.2 6.5 %copy.17 = bf16[1024,8,256]{0,2,1:T(8,128)(2,1)} copy(bf16[1024,8,256]{2,0,1:T(8,128)(2,1)} %bitcast.18) | data formatting | bytes 8388608 | tf_op jit(solution)/shard_map/all_to_all | solution.py:73
  311.7 0.0 all-gather.2.cloned.1.call-done
  311.7 14.6 %fusion.13 = f32[1024,2048]{1,0:T(8,128)} fusion(bf16[1024,2048]{0,1:T(8,128)(2,1)} %bitcast.38, bf16[2048,2048]{1,0:T(8,128)(2,1)} %all-gather.2.cloned.1.call-done), kind=kOutput, calls=%fused_computation.53 | convolution fusion | flops 8589934592 | bytes 20971520 | tf_op jit(solution)/shard_map/dot_general | solution.py:74
  (9 shorter events, 0.1 us)
Async XLA Ops:
  23.9 6.1 %copy-start = (bf16[256,2048]{1,0:T(8,128)(2,1)S(1)}, bf16[256,2048]{1,0:T(8,128)(2,1)}, u32[]{:S(2)}) copy-start(bf16[256,2048]{1,0:T(8,128)(2,1)} %param.11) | copy-start | bytes 3145732
  23.9 6.6 %copy-start.3 = (s32[4]{0:T(128)S(1)}, s32[4]{0:T(128)}, u32[]{:S(2)}) copy-start(s32[4]{0:T(128)} %param.14) | copy-start | bytes 52
  23.9 7.3 %copy-start.5 = (s32[4,2]{0,1:T(2,128)S(1)}, s32[4,2]{0,1:T(2,128)}, u32[]{:S(2)}) copy-start(s32[4,2]{0,1:T(2,128)} %param.15) | copy-start | bytes 100
  23.9 7.3 %copy-start.1 = (bf16[2048]{0:T(1024)(128)(2,1)S(1)}, bf16[2048]{0:T(1024)(128)(2,1)}, u32[]{:S(2)}) copy-start(bf16[2048]{0:T(1024)(128)(2,1)} %param.12) | copy-start | bytes 12292
  23.9 7.3 %copy-start.2 = (bf16[2048]{0:T(1024)(128)(2,1)S(1)}, bf16[2048]{0:T(1024)(128)(2,1)}, u32[]{:S(2)}) copy-start(bf16[2048]{0:T(1024)(128)(2,1)} %param.13) | copy-start | bytes 12292
  23.9 53.9 %all-to-all-start = ((bf16[4,2048,256]{2,1,0:T(8,128)(2,1)}), bf16[4,2048,256]{2,1,0:T(8,128)(2,1)}, u32[]{:S(2)}, u32[]{:S(2)}) async-start(bf16[4,2048,256]{2,1,0:T(8,128)(2,1)} %bitcast.37), calls=%async_computation | async-start | bytes 8388608 | tf_op jit(solution)/shard_map/all_to_all | solution.py:29
  29.3 282.4 %all-gather.2.cloned.1.call-start = ((), (), s32[]{:S(2)}) async-start(), calls=%async_computation.2 | async-start | bytes 9437184 | tf_op jit(solution)/shard_map/all_gather | solution.py:76
  31.3 59.4 %copy-start.4 = (s32[4]{0:T(128)S(1)}, s32[4]{0:T(128)}, u32[]{:S(2)}) copy-start(s32[4]{0:T(128)} %param.16) | copy-start | bytes 52
  114.3 27.0 %collective-permute-start = (bf16[2048,256]{1,0:T(8,128)(2,1)}, bf16[2048,256]{1,0:T(8,128)(2,1)S(1)}, u32[]{:S(2)}, u32[]{:S(2)}) collective-permute-start(bf16[2048,256]{1,0:T(8,128)(2,1)} %get-tuple-element.10), channel_id=1, source_target_pairs={{0,1},{1,2},{2,3},{3,0},{4,5},{5,6},{6,7},{7,4},{8,9},{9,10},{10,1... | collective-permute-start | bytes 3145736 | tf_op jit(solution)/shard_map/ppermute | solution.py:62
  114.3 49.3 %collective-permute-start.2 = (bf16[2048,256]{1,0:T(8,128)(2,1)}, bf16[2048,256]{1,0:T(8,128)(2,1)S(1)}, u32[]{:S(2)}, u32[]{:S(2)}) collective-permute-start(bf16[2048,256]{1,0:T(8,128)(2,1)} %get-tuple-element.10), channel_id=1, source_target_pairs={{1,0},{2,1},{3,2},{0,3},{5,4},{6,5},{7,6},{4,7},{9,8},{10,9},{11,1... | collective-permute-start | bytes 3145736 | tf_op jit(solution)/shard_map/ppermute | solution.py:65
  141.2 44.9 %collective-permute-start.1 = (bf16[2048,256]{1,0:T(8,128)(2,1)S(1)}, bf16[2048,256]{1,0:T(8,128)(2,1)S(1)}, u32[]{:S(2)}, u32[]{:S(2)}) collective-permute-start(bf16[2048,256]{1,0:T(8,128)(2,1)S(1)} %collective-permute-done), channel_id=1, source_target_pairs={{0,1},{1,2},{2,3},{3,0},{4,5},{5,6},{6,7},{7,4},{8,9},{9,10},{10,1... | collective-permute-start | bytes 3145736 | tf_op jit(solution)/shard_map/ppermute | solution.py:62
  194.5 110.7 %all-to-all-start.1 = ((bf16[8,1024,256]{2,1,0:T(8,128)(2,1)}), bf16[8,1024,256]{2,1,0:T(8,128)(2,1)}, u32[]{:S(2)}, u32[]{:S(2)}) async-start(bf16[8,1024,256]{2,1,0:T(8,128)(2,1)} %bitcast.36), calls=%async_computation.1 | async-start | bytes 8388608 | tf_op jit(solution)/shard_map/all_to_all | solution.py:73
Sparse Core Ops, SparseCore 0:
  31.7 85.4 all-gather.1
